TPU v7x, 128 devices: a whole 4x4x4 slice. The times are simulated.
128 devices in a mesh: col: 16 (over x, y), cuts: 8 (over z, core).
Axes of the slice: x: 4, y: 4, z: 4, core: 2. Of those that a mesh axis runs over, the one named last changes fastest.
Arguments:
- layout: int32 [16, 16], P(None, 'col'), may hold values from 0 to 15
- assign: int32 [32, 16], P('cuts', 'col'), may hold values from 0 to 3
- edge: bfloat16 [16, 64, 128], replicated, may hold values from -3 to 3
- gate_left: bfloat16 [16, 16, 64, 128], P('col'), may hold values from -1.5 to 1.5
- gate_right: bfloat16 [16, 16, 64, 128], P('col'), may hold values from -1.5 to 1.5
- phase_angle: float32 [4, 64], replicated, may hold values from -3.140625 to 3.140625
- close: float32 [16, 64, 128], replicated, may hold values from -6 to 6
Outputs:
- slice_amplitude: float32 [32, 2], P('cuts')
- slice_log: float32 [32], P('cuts')
- total_amp: float32 [2], replicated
- top_log: float32 [], replicated
All inputs are finite; a program needn't handle non-finite values. Where the computation divides by a largest or mean magnitude, that divisor is 1e-20 or more.
Results may differ from a plain program's by a relative error of at most 0.0003.
Values sent between devices are 32-bit elements; how exact they have to be, the bound alone decides.
No kernel may reach another device: no remote copies, remote signals or barrier semaphores. Data moves between devices by JAX's collectives and lax.ppermute only.
A program may use at most 64 MiB of HBM per device.

v0:
```python
import math
import jax
import jax.numpy as jnp
from jax import lax
from jax.sharding import Mesh
from jax.sharding import PartitionSpec as P

BLK = 1
COL = ("col_0", "col_1")


def from_behind(value, axis, by):
    length = lax.axis_size(axis)
    pairs = [(i, i + by) for i in range(length) if 0 <= i + by < length]
    return lax.ppermute(value, axis, pairs)


def over_axes(value, axes):
    for axis in axes:
        value = lax.psum(value, axis)
    return value


def from_everyone(value, axis):
    length = lax.axis_size(axis)
    return lax.all_to_all(
        jnp.broadcast_to(value[None], (length, *value.shape)), axis, 0, 0, tiled=True
    )


def of_everyone(value, axis):
    return from_everyone(value, axis).max(axis=0)


def taken_together(value, axis):
    everything = from_everyone(value, axis)
    return jnp.sum(everything, axis=0)


def one_hot(values, count, dtype):
    return (values[..., None] == jnp.arange(count, dtype=jnp.int32)).astype(dtype)


def sweep_column(board, left_sel, right_sel, cosine, sine):
    width = board.shape[-2]
    below = jnp.concatenate([board[:, 1:], jnp.zeros_like(board[:, :1])], axis=1)
    mixed = board + 0.5 * below
    left_four = left_sel.reshape(left_sel.shape[0], width, 2, width)
    stacked = jnp.einsum("rpka,srab->srkpb", left_four, mixed, precision=lax.Precision.HIGHEST)
    former = stacked[:, :, 0]
    latter = stacked[:, :, 1]
    real_part = former[..., :width] - latter[..., width:]
    imag_part = former[..., width:] + latter[..., :width]
    from_real = jnp.einsum("srab,rbq->sraq", real_part, right_sel, precision=lax.Precision.HIGHEST)
    from_imag = jnp.einsum("srab,rbq->sraq", imag_part, right_sel, precision=lax.Precision.HIGHEST)
    out_real = from_real[..., :width] - from_imag[..., width:]
    out_imag = from_real[..., width:] + from_imag[..., :width]
    cos_rows = cosine[:, None, None, :]
    sin_rows = sine[:, None, None, :]
    turned_real = out_real * cos_rows - out_imag * sin_rows
    turned_imag = out_real * sin_rows + out_imag * cos_rows
    peaks = jnp.maximum(
        jnp.max(jnp.abs(turned_real), axis=(1, 2, 3)), jnp.max(jnp.abs(turned_imag), axis=(1, 2, 3))
    )
    peaks = jnp.maximum(peaks, 1.0)
    board = jnp.concatenate([turned_real, turned_imag], -1) / peaks[:, None, None, None]
    return (board, jnp.log(peaks))


def amplitude(board, close):
    width = close.shape[-1] // 2
    b_real = board[..., :width]
    b_imag = board[..., width:]
    c_real = close[..., :width]
    c_imag = close[..., width:]
    factor = 1.0 / math.sqrt(close.shape[0] * width * width)
    amp_real = jnp.sum(b_real * c_real - b_imag * c_imag, axis=(1, 2, 3)) * factor
    amp_imag = jnp.sum(b_real * c_imag + b_imag * c_real, axis=(1, 2, 3)) * factor
    return jnp.stack([amp_real, amp_imag], -1)


def body(layout, assign, edge, gate_left, gate_right, phase_angle, close):
    sections = lax.axis_size(COL)
    place = lax.axis_index(COL)
    kinds = gate_left.shape[1]
    values = phase_angle.shape[0]
    per_device = assign.shape[0]
    group = BLK
    groups = per_device // group
    row_hot = one_hot(layout.T, kinds, jnp.bfloat16)
    left_all = jnp.einsum("crg,cgpq->crpq", row_hot, gate_left, preferred_element_type=jnp.float32)
    right_all = jnp.einsum(
        "crg,cgpq->crpq", row_hot, gate_right, preferred_element_type=jnp.float32
    )
    cos_table = jnp.cos(phase_angle)
    sin_table = jnp.sin(phase_angle)
    start_board = edge.astype(jnp.float32)[None]

    def run_columns(board, assign_group):
        value_hot = one_hot(assign_group, values, jnp.float32)
        cos_sel = jnp.einsum("scq,qb->scb", value_hot, cos_table, precision=lax.Precision.HIGHEST)
        sin_sel = jnp.einsum("scq,qb->scb", value_hot, sin_table, precision=lax.Precision.HIGHEST)
        board, scales = sweep_column(board, left_all[0], right_all[0], cos_sel[:, 0], sin_sel[:, 0])
        return (board, scales)

    def section(step, carry):
        held_board, amps, logs = carry
        index = step - place
        valid = jnp.logical_and(index >= 0, index < groups)
        safe = jnp.clip(index, 0, groups - 1)
        first = place == 0
        board = jnp.where(first, start_board, held_board)
        assign_group = lax.dynamic_slice_in_dim(assign, safe * group, group, 0)
        board, scales = lax.cond(
            valid,
            lambda: run_columns(board, assign_group),
            lambda: (board, jnp.zeros((group,), jnp.float32)),
        )
        keep = jnp.logical_and(valid, place == sections - 1)
        amps = jnp.where(
            keep,
            lax.dynamic_update_slice_in_dim(amps, amplitude(board, close), safe * group, 0),
            amps,
        )
        logs = jnp.where(
            valid, lax.dynamic_update_slice_in_dim(logs, scales, safe * group, 0), logs
        )
        held_board = from_behind(board, COL, 1)
        return (held_board, amps, logs)

    initial = (
        start_board,
        jnp.zeros((per_device, 2), jnp.float32),
        jnp.zeros((per_device,), jnp.float32),
    )
    unused_board, amps, logs = lax.fori_loop(0, sections + groups - 1, section, initial)
    amps, logs = (over_axes(amps, COL), over_axes(logs, COL))
    local_top = jnp.max(logs)
    top_log = of_everyone(local_top, "cuts")
    partial_sum = jnp.sum(amps * jnp.exp(logs - top_log)[:, None], axis=0)
    total_amp = taken_together(partial_sum, "cuts")
    return (amps, logs, total_amp, top_log)


def solution(mesh):
    split = Mesh(mesh.devices.reshape(4, 4, mesh.shape["cuts"]), ("col_0", "col_1", "cuts"))
    placed = (
        P(None, COL),
        P("cuts", COL),
        P(),
        P(COL, None, None, None),
        P(COL, None, None, None),
        P(),
        P(),
    )
    return jax.shard_map(
        body,
        mesh=split,
        in_specs=placed,
        out_specs=(P("cuts", None), P("cuts"), P(), P()),
        check_vma=False,
    )
```

profile of v0, /device:TPU:1, one launch (start us, length us, event | category | flops | bytes accessed | tf_op | source)
XLA Modules:
  0.0 458.8 jit_solution(4643942819988756618)
XLA Ops:
  6.2 341.0 %while.18 = (s32[]{:T(128)}, f32[1,16,64,128]{3,2,1,0:T(8,128)S(1)}, f32[4,2]{0,1:T(2,128)S(1)}, f32[4]{0:T(128)S(1)}, s32[]{:T(128)}, /*index=5*/pred[]{:T(512)...) while((s32[]{:T(128)}, ...), condition=%wide.region_7.8_spmd, body=%wide.region_0.7_spmd.sunk | while | flops 404756480 | bytes 22449744 | solution.py:136
  7.0 8.9 %conditional.2 = (f32[1,16,64,128]{3,2,1,0:T(8,128)S(1)}, f32[1]{0:T(128)}) conditional(s32[]{:T(128)} %convert_element_type.12, f32[1,16,64,128]{3,2,1,0:T(8,128)S(1)} %broadcast_select_fusion.2, (f32[1,16,64,128]{3,2,1,0:T(8,128)S(1)}, f32[1,16,64,128]{3,2,1,0:T(8,128)}, f32[1,16,64,128]{3,2,1,0:T(8,128)S(1)}, s32[4,1]{0,1:T(1,128)S(1)}, s32[]{:T(128)}, ...), branch_computations={%region_1.1_spmd, %region_2.4_spmd} | conditional | flops 404101120 | bytes 13536336 | solution.py:114
  19.8 7.7 %collective-permute-done = f32[1,16,64,128]{3,2,1,0:T(8,128)S(1)} collective-permute-done((f32[1,16,64,128]{3,2,1,0:T(8,128)S(1)}, f32[1,16,64,128]{3,2,1,0:T(8,128)S(1)}, u32[]{:S(2)}, u32[]{:S(2)}) %collective-permute-start) | collective-permute-done | bytes 524320 | tf_op jit(solution)/shard_map/while/body/eval_jaxpr/ppermute | solution.py:15
  28.3 8.9 %conditional.2 = (f32[1,16,64,128]{3,2,1,0:T(8,128)S(1)}, f32[1]{0:T(128)}) conditional(s32[]{:T(128)} %convert_element_type.12, f32[1,16,64,128]{3,2,1,0:T(8,128)S(1)} %broadcast_select_fusion.2, (f32[1,16,64,128]{3,2,1,0:T(8,128)S(1)}, f32[1,16,64,128]{3,2,1,0:T(8,128)}, f32[1,16,64,128]{3,2,1,0:T(8,128)S(1)}, s32[4,1]{0,1:T(1,128)S(1)}, s32[]{:T(128)}, ...), branch_computations={%region_1.1_spmd, %region_2.4_spmd} | conditional | flops 404101120 | bytes 13536336 | solution.py:114
  43.9 6.7 %collective-permute-done = f32[1,16,64,128]{3,2,1,0:T(8,128)S(1)} collective-permute-done((f32[1,16,64,128]{3,2,1,0:T(8,128)S(1)}, f32[1,16,64,128]{3,2,1,0:T(8,128)S(1)}, u32[]{:S(2)}, u32[]{:S(2)}) %collective-permute-start) | collective-permute-done | bytes 524320 | tf_op jit(solution)/shard_map/while/body/eval_jaxpr/ppermute | solution.py:15
  51.4 8.9 %conditional.2 = (f32[1,16,64,128]{3,2,1,0:T(8,128)S(1)}, f32[1]{0:T(128)}) conditional(s32[]{:T(128)} %convert_element_type.12, f32[1,16,64,128]{3,2,1,0:T(8,128)S(1)} %broadcast_select_fusion.2, (f32[1,16,64,128]{3,2,1,0:T(8,128)S(1)}, f32[1,16,64,128]{3,2,1,0:T(8,128)}, f32[1,16,64,128]{3,2,1,0:T(8,128)S(1)}, s32[4,1]{0,1:T(1,128)S(1)}, s32[]{:T(128)}, ...), branch_computations={%region_1.1_spmd, %region_2.4_spmd} | conditional | flops 404101120 | bytes 13536336 | solution.py:114
  67.0 5.9 %collective-permute-done = f32[1,16,64,128]{3,2,1,0:T(8,128)S(1)} collective-permute-done((f32[1,16,64,128]{3,2,1,0:T(8,128)S(1)}, f32[1,16,64,128]{3,2,1,0:T(8,128)S(1)}, u32[]{:S(2)}, u32[]{:S(2)}) %collective-permute-start) | collective-permute-done | bytes 524320 | tf_op jit(solution)/shard_map/while/body/eval_jaxpr/ppermute | solution.py:15
  73.8 8.9 %conditional.2 = (f32[1,16,64,128]{3,2,1,0:T(8,128)S(1)}, f32[1]{0:T(128)}) conditional(s32[]{:T(128)} %convert_element_type.12, f32[1,16,64,128]{3,2,1,0:T(8,128)S(1)} %broadcast_select_fusion.2, (f32[1,16,64,128]{3,2,1,0:T(8,128)S(1)}, f32[1,16,64,128]{3,2,1,0:T(8,128)}, f32[1,16,64,128]{3,2,1,0:T(8,128)S(1)}, s32[4,1]{0,1:T(1,128)S(1)}, s32[]{:T(128)}, ...), branch_computations={%region_1.1_spmd, %region_2.4_spmd} | conditional | flops 404101120 | bytes 13536336 | solution.py:114
  89.4 5.0 %collective-permute-done = f32[1,16,64,128]{3,2,1,0:T(8,128)S(1)} collective-permute-done((f32[1,16,64,128]{3,2,1,0:T(8,128)S(1)}, f32[1,16,64,128]{3,2,1,0:T(8,128)S(1)}, u32[]{:S(2)}, u32[]{:S(2)}) %collective-permute-start) | collective-permute-done | bytes 524320 | tf_op jit(solution)/shard_map/while/body/eval_jaxpr/ppermute | solution.py:15
  95.2 13.1 %collective-permute-start = (f32[1,16,64,128]{3,2,1,0:T(8,128)S(1)}, f32[1,16,64,128]{3,2,1,0:T(8,128)S(1)}, u32[]{:S(2)}, u32[]{:S(2)}) collective-permute-start(f32[1,16,64,128]{3,2,1,0:T(8,128)S(1)} %get-tuple-element.477), channel_id=1, source_target_pairs={{0,8},{8,16},{16,24},{24,32},{32,40},{40,48},{48,56},{56,64},{64,7... | collective-permute-start | bytes 1572872 | tf_op jit(solution)/shard_map/while/body/eval_jaxpr/ppermute | solution.py:15
  126.8 12.0 %collective-permute-start = (f32[1,16,64,128]{3,2,1,0:T(8,128)S(1)}, f32[1,16,64,128]{3,2,1,0:T(8,128)S(1)}, u32[]{:S(2)}, u32[]{:S(2)}) collective-permute-start(f32[1,16,64,128]{3,2,1,0:T(8,128)S(1)} %get-tuple-element.477), channel_id=1, source_target_pairs={{0,8},{8,16},{16,24},{24,32},{32,40},{40,48},{48,56},{56,64},{64,7... | collective-permute-start | bytes 1572872 | tf_op jit(solution)/shard_map/while/body/eval_jaxpr/ppermute | solution.py:15
  158.0 13.7 %collective-permute-start = (f32[1,16,64,128]{3,2,1,0:T(8,128)S(1)}, f32[1,16,64,128]{3,2,1,0:T(8,128)S(1)}, u32[]{:S(2)}, u32[]{:S(2)}) collective-permute-start(f32[1,16,64,128]{3,2,1,0:T(8,128)S(1)} %get-tuple-element.477), channel_id=1, source_target_pairs={{0,8},{8,16},{16,24},{24,32},{32,40},{40,48},{48,56},{56,64},{64,7... | collective-permute-start | bytes 1572872 | tf_op jit(solution)/shard_map/while/body/eval_jaxpr/ppermute | solution.py:15
  178.6 6.2 %collective-permute-start = (f32[1,16,64,128]{3,2,1,0:T(8,128)S(1)}, f32[1,16,64,128]{3,2,1,0:T(8,128)S(1)}, u32[]{:S(2)}, u32[]{:S(2)}) collective-permute-start(f32[1,16,64,128]{3,2,1,0:T(8,128)S(1)} %get-tuple-element.477), channel_id=1, source_target_pairs={{0,8},{8,16},{16,24},{24,32},{32,40},{40,48},{48,56},{56,64},{64,7... | collective-permute-start | bytes 1572872 | tf_op jit(solution)/shard_map/while/body/eval_jaxpr/ppermute | solution.py:15
  191.8 14.8 %collective-permute-start = (f32[1,16,64,128]{3,2,1,0:T(8,128)S(1)}, f32[1,16,64,128]{3,2,1,0:T(8,128)S(1)}, u32[]{:S(2)}, u32[]{:S(2)}) collective-permute-start(f32[1,16,64,128]{3,2,1,0:T(8,128)S(1)} %get-tuple-element.477), channel_id=1, source_target_pairs={{0,8},{8,16},{16,24},{24,32},{32,40},{40,48},{48,56},{56,64},{64,7... | collective-permute-start | bytes 1572872 | tf_op jit(solution)/shard_map/while/body/eval_jaxpr/ppermute | solution.py:15
  213.5 8.1 %collective-permute-start = (f32[1,16,64,128]{3,2,1,0:T(8,128)S(1)}, f32[1,16,64,128]{3,2,1,0:T(8,128)S(1)}, u32[]{:S(2)}, u32[]{:S(2)}) collective-permute-start(f32[1,16,64,128]{3,2,1,0:T(8,128)S(1)} %get-tuple-element.477), channel_id=1, source_target_pairs={{0,8},{8,16},{16,24},{24,32},{32,40},{40,48},{48,56},{56,64},{64,7... | collective-permute-start | bytes 1572872 | tf_op jit(solution)/shard_map/while/body/eval_jaxpr/ppermute | solution.py:15
  224.1 5.9 %collective-permute-done = f32[1,16,64,128]{3,2,1,0:T(8,128)S(1)} collective-permute-done((f32[1,16,64,128]{3,2,1,0:T(8,128)S(1)}, f32[1,16,64,128]{3,2,1,0:T(8,128)S(1)}, u32[]{:S(2)}, u32[]{:S(2)}) %collective-permute-start) | collective-permute-done | bytes 524320 | tf_op jit(solution)/shard_map/while/body/eval_jaxpr/ppermute | solution.py:15
  237.7 6.6 %collective-permute-done = f32[1,16,64,128]{3,2,1,0:T(8,128)S(1)} collective-permute-done((f32[1,16,64,128]{3,2,1,0:T(8,128)S(1)}, f32[1,16,64,128]{3,2,1,0:T(8,128)S(1)}, u32[]{:S(2)}, u32[]{:S(2)}) %collective-permute-start) | collective-permute-done | bytes 524320 | tf_op jit(solution)/shard_map/while/body/eval_jaxpr/ppermute | solution.py:15
  245.1 17.0 %collective-permute-start = (f32[1,16,64,128]{3,2,1,0:T(8,128)S(1)}, f32[1,16,64,128]{3,2,1,0:T(8,128)S(1)}, u32[]{:S(2)}, u32[]{:S(2)}) collective-permute-start(f32[1,16,64,128]{3,2,1,0:T(8,128)S(1)} %get-tuple-element.477), channel_id=1, source_target_pairs={{0,8},{8,16},{16,24},{24,32},{32,40},{40,48},{48,56},{56,64},{64,7... | collective-permute-start | bytes 1572872 | tf_op jit(solution)/shard_map/while/body/eval_jaxpr/ppermute | solution.py:15
  264.6 8.6 %collective-permute-done = f32[1,16,64,128]{3,2,1,0:T(8,128)S(1)} collective-permute-done((f32[1,16,64,128]{3,2,1,0:T(8,128)S(1)}, f32[1,16,64,128]{3,2,1,0:T(8,128)S(1)}, u32[]{:S(2)}, u32[]{:S(2)}) %collective-permute-start) | collective-permute-done | bytes 524320 | tf_op jit(solution)/shard_map/while/body/eval_jaxpr/ppermute | solution.py:15
  274.0 6.2 %collective-permute-start = (f32[1,16,64,128]{3,2,1,0:T(8,128)S(1)}, f32[1,16,64,128]{3,2,1,0:T(8,128)S(1)}, u32[]{:S(2)}, u32[]{:S(2)}) collective-permute-start(f32[1,16,64,128]{3,2,1,0:T(8,128)S(1)} %get-tuple-element.477), channel_id=1, source_target_pairs={{0,8},{8,16},{16,24},{24,32},{32,40},{40,48},{48,56},{56,64},{64,7... | collective-permute-start | bytes 1572872 | tf_op jit(solution)/shard_map/while/body/eval_jaxpr/ppermute | solution.py:15
  282.8 7.4 %collective-permute-done = f32[1,16,64,128]{3,2,1,0:T(8,128)S(1)} collective-permute-done((f32[1,16,64,128]{3,2,1,0:T(8,128)S(1)}, f32[1,16,64,128]{3,2,1,0:T(8,128)S(1)}, u32[]{:S(2)}, u32[]{:S(2)}) %collective-permute-start) | collective-permute-done | bytes 524320 | tf_op jit(solution)/shard_map/while/body/eval_jaxpr/ppermute | solution.py:15
  291.0 5.1 %collective-permute-start = (f32[1,16,64,128]{3,2,1,0:T(8,128)S(1)}, f32[1,16,64,128]{3,2,1,0:T(8,128)S(1)}, u32[]{:S(2)}, u32[]{:S(2)}) collective-permute-start(f32[1,16,64,128]{3,2,1,0:T(8,128)S(1)} %get-tuple-element.477), channel_id=1, source_target_pairs={{0,8},{8,16},{16,24},{24,32},{32,40},{40,48},{48,56},{56,64},{64,7... | collective-permute-start | bytes 1572872 | tf_op jit(solution)/shard_map/while/body/eval_jaxpr/ppermute | solution.py:15
  298.6 6.3 %collective-permute-done = f32[1,16,64,128]{3,2,1,0:T(8,128)S(1)} collective-permute-done((f32[1,16,64,128]{3,2,1,0:T(8,128)S(1)}, f32[1,16,64,128]{3,2,1,0:T(8,128)S(1)}, u32[]{:S(2)}, u32[]{:S(2)}) %collective-permute-start) | collective-permute-done | bytes 524320 | tf_op jit(solution)/shard_map/while/body/eval_jaxpr/ppermute | solution.py:15
  305.7 6.2 %collective-permute-start = (f32[1,16,64,128]{3,2,1,0:T(8,128)S(1)}, f32[1,16,64,128]{3,2,1,0:T(8,128)S(1)}, u32[]{:S(2)}, u32[]{:S(2)}) collective-permute-start(f32[1,16,64,128]{3,2,1,0:T(8,128)S(1)} %get-tuple-element.477), channel_id=1, source_target_pairs={{0,8},{8,16},{16,24},{24,32},{32,40},{40,48},{48,56},{56,64},{64,7... | collective-permute-start | bytes 1572872 | tf_op jit(solution)/shard_map/while/body/eval_jaxpr/ppermute | solution.py:15
  314.5 5.4 %collective-permute-done = f32[1,16,64,128]{3,2,1,0:T(8,128)S(1)} collective-permute-done((f32[1,16,64,128]{3,2,1,0:T(8,128)S(1)}, f32[1,16,64,128]{3,2,1,0:T(8,128)S(1)}, u32[]{:S(2)}, u32[]{:S(2)}) %collective-permute-start) | collective-permute-done | bytes 524320 | tf_op jit(solution)/shard_map/while/body/eval_jaxpr/ppermute | solution.py:15
  320.7 6.2 %collective-permute-start = (f32[1,16,64,128]{3,2,1,0:T(8,128)S(1)}, f32[1,16,64,128]{3,2,1,0:T(8,128)S(1)}, u32[]{:S(2)}, u32[]{:S(2)}) collective-permute-start(f32[1,16,64,128]{3,2,1,0:T(8,128)S(1)} %get-tuple-element.477), channel_id=1, source_target_pairs={{0,8},{8,16},{16,24},{24,32},{32,40},{40,48},{48,56},{56,64},{64,7... | collective-permute-start | bytes 1572872 | tf_op jit(solution)/shard_map/while/body/eval_jaxpr/ppermute | solution.py:15
  329.5 4.6 collective-permute-done
  334.9 6.2 %collective-permute-start = (f32[1,16,64,128]{3,2,1,0:T(8,128)S(1)}, f32[1,16,64,128]{3,2,1,0:T(8,128)S(1)}, u32[]{:S(2)}, u32[]{:S(2)}) collective-permute-start(f32[1,16,64,128]{3,2,1,0:T(8,128)S(1)} %get-tuple-element.477), channel_id=1, source_target_pairs={{0,8},{8,16},{16,24},{24,32},{32,40},{40,48},{48,56},{56,64},{64,7... | collective-permute-start | bytes 1572872 | tf_op jit(solution)/shard_map/while/body/eval_jaxpr/ppermute | solution.py:15
  347.2 53.0 %all-reduce.2 = (f32[4,2]{0,1:T(2,128)S(1)}, f32[4]{0:T(128)S(1)}) all-reduce(f32[4,2]{0,1:T(2,128)S(1)} %get-tuple-element.300, f32[4]{0:T(128)S(1)} %get-tuple-element.301), channel_id=1, replica_groups=mesh['col_0'=4,'col_1'=4,'cuts'=8] {'col_0'}, use_global_device_ids=true, to_apply=%region_8.9 | all-reduce | flops 12 | bytes 96 | tf_op jit(solution)/shard_map/psum | solution.py:20
  400.2 12.3 %all-reduce.1 = (f32[4,2]{0,1:T(2,128)S(1)}, f32[4]{0:T(128)S(1)}) all-reduce(f32[4,2]{0,1:T(2,128)S(1)} %get-tuple-element.376, f32[4]{0:T(128)S(1)} %get-tuple-element.377), channel_id=1, replica_groups=mesh['col_0'=4,'col_1'=4,'cuts'=8] {'col_1'}, use_global_device_ids=true, to_apply=%region_9.10 | all-reduce | flops 12 | bytes 96 | tf_op jit(solution)/shard_map/psum | solution.py:20
  413.7 35.5 %all_to_all.12 = f32[8,1,1]{2,1,0:T(1,128)S(1)} all-to-all(f32[8,1,1]{2,1,0:T(1,128)S(1)} %broadcast_in_dim.43), channel_id=1, replica_groups=mesh['col_0'=4,'col_1'=4,'cuts'=8] {'cuts'}, dimensions={0} | all-to-all | bytes 64 | tf_op jit(solution)/shard_map/all_to_all | solution.py:26
  450.6 7.6 %all_to_all.13 = f32[8,1,2]{2,1,0:T(1,128)S(1)} all-to-all(f32[8,1,2]{2,1,0:T(1,128)S(1)} %broadcast_in_dim.44), channel_id=1, replica_groups=mesh['col_0'=4,'col_1'=4,'cuts'=8] {'cuts'}, dimensions={0} | all-to-all | bytes 128 | tf_op jit(solution)/shard_map/all_to_all | solution.py:26
  (279 shorter events, 135.8 us)
Async XLA Ops:
  16.0 11.5 %collective-permute-start = (f32[1,16,64,128]{3,2,1,0:T(8,128)S(1)}, f32[1,16,64,128]{3,2,1,0:T(8,128)S(1)}, u32[]{:S(2)}, u32[]{:S(2)}) collective-permute-start(f32[1,16,64,128]{3,2,1,0:T(8,128)S(1)} %get-tuple-element.477), channel_id=1, source_target_pairs={{0,8},{8,16},{16,24},{24,32},{32,40},{40,48},{48,56},{56,64},{64,7... | collective-permute-start | bytes 1572872 | tf_op jit(solution)/shard_map/while/body/eval_jaxpr/ppermute | solution.py:15
  17.3 10.1 %copy-start.3 = (f32[1,16,64,128]{3,2,1,0:T(8,128)S(1)}, f32[1,16,64,128]{3,2,1,0:T(8,128)}, u32[]{:S(2)}) copy-start(f32[1,16,64,128]{3,2,1,0:T(8,128)} %copy-done.2) | copy-start | bytes 1572868 | tf_op jit(solution)/shard_map/while
  37.2 13.4 %collective-permute-start = (f32[1,16,64,128]{3,2,1,0:T(8,128)S(1)}, f32[1,16,64,128]{3,2,1,0:T(8,128)S(1)}, u32[]{:S(2)}, u32[]{:S(2)}) collective-permute-start(f32[1,16,64,128]{3,2,1,0:T(8,128)S(1)} %get-tuple-element.477), channel_id=1, source_target_pairs={{0,8},{8,16},{16,24},{24,32},{32,40},{40,48},{48,56},{56,64},{64,7... | collective-permute-start | bytes 1572872 | tf_op jit(solution)/shard_map/while/body/eval_jaxpr/ppermute | solution.py:15
  41.3 9.3 %copy-start.3 = (f32[1,16,64,128]{3,2,1,0:T(8,128)S(1)}, f32[1,16,64,128]{3,2,1,0:T(8,128)}, u32[]{:S(2)}) copy-start(f32[1,16,64,128]{3,2,1,0:T(8,128)} %copy-done.2) | copy-start | bytes 1572868 | tf_op jit(solution)/shard_map/while
  60.4 12.6 %collective-permute-start = (f32[1,16,64,128]{3,2,1,0:T(8,128)S(1)}, f32[1,16,64,128]{3,2,1,0:T(8,128)S(1)}, u32[]{:S(2)}, u32[]{:S(2)}) collective-permute-start(f32[1,16,64,128]{3,2,1,0:T(8,128)S(1)} %get-tuple-element.477), channel_id=1, source_target_pairs={{0,8},{8,16},{16,24},{24,32},{32,40},{40,48},{48,56},{56,64},{64,7... | collective-permute-start | bytes 1572872 | tf_op jit(solution)/shard_map/while/body/eval_jaxpr/ppermute | solution.py:15
  64.5 8.4 %copy-start.3 = (f32[1,16,64,128]{3,2,1,0:T(8,128)S(1)}, f32[1,16,64,128]{3,2,1,0:T(8,128)}, u32[]{:S(2)}) copy-start(f32[1,16,64,128]{3,2,1,0:T(8,128)} %copy-done.2) | copy-start | bytes 1572868 | tf_op jit(solution)/shard_map/while
  82.7 11.7 %collective-permute-start = (f32[1,16,64,128]{3,2,1,0:T(8,128)S(1)}, f32[1,16,64,128]{3,2,1,0:T(8,128)S(1)}, u32[]{:S(2)}, u32[]{:S(2)}) collective-permute-start(f32[1,16,64,128]{3,2,1,0:T(8,128)S(1)} %get-tuple-element.477), channel_id=1, source_target_pairs={{0,8},{8,16},{16,24},{24,32},{32,40},{40,48},{48,56},{56,64},{64,7... | collective-permute-start | bytes 1572872 | tf_op jit(solution)/shard_map/while/body/eval_jaxpr/ppermute | solution.py:15
  86.8 7.6 %copy-start.3 = (f32[1,16,64,128]{3,2,1,0:T(8,128)S(1)}, f32[1,16,64,128]{3,2,1,0:T(8,128)}, u32[]{:S(2)}) copy-start(f32[1,16,64,128]{3,2,1,0:T(8,128)} %copy-done.2) | copy-start | bytes 1572868 | tf_op jit(solution)/shard_map/while
  95.2 19.8 %collective-permute-start = (f32[1,16,64,128]{3,2,1,0:T(8,128)S(1)}, f32[1,16,64,128]{3,2,1,0:T(8,128)S(1)}, u32[]{:S(2)}, u32[]{:S(2)}) collective-permute-start(f32[1,16,64,128]{3,2,1,0:T(8,128)S(1)} %get-tuple-element.477), channel_id=1, source_target_pairs={{0,8},{8,16},{16,24},{24,32},{32,40},{40,48},{48,56},{56,64},{64,7... | collective-permute-start | bytes 1572872 | tf_op jit(solution)/shard_map/while/body/eval_jaxpr/ppermute | solution.py:15
  115.8 10.2 %collective-permute-start = (f32[1,16,64,128]{3,2,1,0:T(8,128)S(1)}, f32[1,16,64,128]{3,2,1,0:T(8,128)S(1)}, u32[]{:S(2)}, u32[]{:S(2)}) collective-permute-start(f32[1,16,64,128]{3,2,1,0:T(8,128)S(1)} %get-tuple-element.477), channel_id=1, source_target_pairs={{0,8},{8,16},{16,24},{24,32},{32,40},{40,48},{48,56},{56,64},{64,7... | collective-permute-start | bytes 1572872 | tf_op jit(solution)/shard_map/while/body/eval_jaxpr/ppermute | solution.py:15
  126.8 18.1 %collective-permute-start = (f32[1,16,64,128]{3,2,1,0:T(8,128)S(1)}, f32[1,16,64,128]{3,2,1,0:T(8,128)S(1)}, u32[]{:S(2)}, u32[]{:S(2)}) collective-permute-start(f32[1,16,64,128]{3,2,1,0:T(8,128)S(1)} %get-tuple-element.477), channel_id=1, source_target_pairs={{0,8},{8,16},{16,24},{24,32},{32,40},{40,48},{48,56},{56,64},{64,7... | collective-permute-start | bytes 1572872 | tf_op jit(solution)/shard_map/while/body/eval_jaxpr/ppermute | solution.py:15
  145.8 11.4 %collective-permute-start = (f32[1,16,64,128]{3,2,1,0:T(8,128)S(1)}, f32[1,16,64,128]{3,2,1,0:T(8,128)S(1)}, u32[]{:S(2)}, u32[]{:S(2)}) collective-permute-start(f32[1,16,64,128]{3,2,1,0:T(8,128)S(1)} %get-tuple-element.477), channel_id=1, source_target_pairs={{0,8},{8,16},{16,24},{24,32},{32,40},{40,48},{48,56},{56,64},{64,7... | collective-permute-start | bytes 1572872 | tf_op jit(solution)/shard_map/while/body/eval_jaxpr/ppermute | solution.py:15
  158.0 19.8 %collective-permute-start = (f32[1,16,64,128]{3,2,1,0:T(8,128)S(1)}, f32[1,16,64,128]{3,2,1,0:T(8,128)S(1)}, u32[]{:S(2)}, u32[]{:S(2)}) collective-permute-start(f32[1,16,64,128]{3,2,1,0:T(8,128)S(1)} %get-tuple-element.477), channel_id=1, source_target_pairs={{0,8},{8,16},{16,24},{24,32},{32,40},{40,48},{48,56},{56,64},{64,7... | collective-permute-start | bytes 1572872 | tf_op jit(solution)/shard_map/while/body/eval_jaxpr/ppermute | solution.py:15
  178.6 12.4 %collective-permute-start = (f32[1,16,64,128]{3,2,1,0:T(8,128)S(1)}, f32[1,16,64,128]{3,2,1,0:T(8,128)S(1)}, u32[]{:S(2)}, u32[]{:S(2)}) collective-permute-start(f32[1,16,64,128]{3,2,1,0:T(8,128)S(1)} %get-tuple-element.477), channel_id=1, source_target_pairs={{0,8},{8,16},{16,24},{24,32},{32,40},{40,48},{48,56},{56,64},{64,7... | collective-permute-start | bytes 1572872 | tf_op jit(solution)/shard_map/while/body/eval_jaxpr/ppermute | solution.py:15
  191.8 20.9 %collective-permute-start = (f32[1,16,64,128]{3,2,1,0:T(8,128)S(1)}, f32[1,16,64,128]{3,2,1,0:T(8,128)S(1)}, u32[]{:S(2)}, u32[]{:S(2)}) collective-permute-start(f32[1,16,64,128]{3,2,1,0:T(8,128)S(1)} %get-tuple-element.477), channel_id=1, source_target_pairs={{0,8},{8,16},{16,24},{24,32},{32,40},{40,48},{48,56},{56,64},{64,7... | collective-permute-start | bytes 1572872 | tf_op jit(solution)/shard_map/while/body/eval_jaxpr/ppermute | solution.py:15
  213.5 16.5 %collective-permute-start = (f32[1,16,64,128]{3,2,1,0:T(8,128)S(1)}, f32[1,16,64,128]{3,2,1,0:T(8,128)S(1)}, u32[]{:S(2)}, u32[]{:S(2)}) collective-permute-start(f32[1,16,64,128]{3,2,1,0:T(8,128)S(1)} %get-tuple-element.477), channel_id=1, source_target_pairs={{0,8},{8,16},{16,24},{24,32},{32,40},{40,48},{48,56},{56,64},{64,7... | collective-permute-start | bytes 1572872 | tf_op jit(solution)/shard_map/while/body/eval_jaxpr/ppermute | solution.py:15
  221.6 8.4 %copy-start.3 = (f32[1,16,64,128]{3,2,1,0:T(8,128)S(1)}, f32[1,16,64,128]{3,2,1,0:T(8,128)}, u32[]{:S(2)}) copy-start(f32[1,16,64,128]{3,2,1,0:T(8,128)} %copy-done.2) | copy-start | bytes 1572868 | tf_op jit(solution)/shard_map/while
  230.9 13.4 %collective-permute-start = (f32[1,16,64,128]{3,2,1,0:T(8,128)S(1)}, f32[1,16,64,128]{3,2,1,0:T(8,128)S(1)}, u32[]{:S(2)}, u32[]{:S(2)}) collective-permute-start(f32[1,16,64,128]{3,2,1,0:T(8,128)S(1)} %get-tuple-element.477), channel_id=1, source_target_pairs={{0,8},{8,16},{16,24},{24,32},{32,40},{40,48},{48,56},{56,64},{64,7... | collective-permute-start | bytes 1572872 | tf_op jit(solution)/shard_map/while/body/eval_jaxpr/ppermute | solution.py:15
  235.1 9.2 %copy-start.3 = (f32[1,16,64,128]{3,2,1,0:T(8,128)S(1)}, f32[1,16,64,128]{3,2,1,0:T(8,128)}, u32[]{:S(2)}) copy-start(f32[1,16,64,128]{3,2,1,0:T(8,128)} %copy-done.2) | copy-start | bytes 1572868 | tf_op jit(solution)/shard_map/while
  245.1 28.1 %collective-permute-start = (f32[1,16,64,128]{3,2,1,0:T(8,128)S(1)}, f32[1,16,64,128]{3,2,1,0:T(8,128)S(1)}, u32[]{:S(2)}, u32[]{:S(2)}) collective-permute-start(f32[1,16,64,128]{3,2,1,0:T(8,128)S(1)} %get-tuple-element.477), channel_id=1, source_target_pairs={{0,8},{8,16},{16,24},{24,32},{32,40},{40,48},{48,56},{56,64},{64,7... | collective-permute-start | bytes 1572872 | tf_op jit(solution)/shard_map/while/body/eval_jaxpr/ppermute | solution.py:15
  262.1 11.1 %copy-start.3 = (f32[1,16,64,128]{3,2,1,0:T(8,128)S(1)}, f32[1,16,64,128]{3,2,1,0:T(8,128)}, u32[]{:S(2)}) copy-start(f32[1,16,64,128]{3,2,1,0:T(8,128)} %copy-done.2) | copy-start | bytes 1572868 | tf_op jit(solution)/shard_map/while
  274.0 16.1 %collective-permute-start = (f32[1,16,64,128]{3,2,1,0:T(8,128)S(1)}, f32[1,16,64,128]{3,2,1,0:T(8,128)S(1)}, u32[]{:S(2)}, u32[]{:S(2)}) collective-permute-start(f32[1,16,64,128]{3,2,1,0:T(8,128)S(1)} %get-tuple-element.477), channel_id=1, source_target_pairs={{0,8},{8,16},{16,24},{24,32},{32,40},{40,48},{48,56},{56,64},{64,7... | collective-permute-start | bytes 1572872 | tf_op jit(solution)/shard_map/while/body/eval_jaxpr/ppermute | solution.py:15
  280.2 10.0 %copy-start.3 = (f32[1,16,64,128]{3,2,1,0:T(8,128)S(1)}, f32[1,16,64,128]{3,2,1,0:T(8,128)}, u32[]{:S(2)}) copy-start(f32[1,16,64,128]{3,2,1,0:T(8,128)} %copy-done.2) | copy-start | bytes 1572868 | tf_op jit(solution)/shard_map/while
  291.0 13.9 %collective-permute-start = (f32[1,16,64,128]{3,2,1,0:T(8,128)S(1)}, f32[1,16,64,128]{3,2,1,0:T(8,128)S(1)}, u32[]{:S(2)}, u32[]{:S(2)}) collective-permute-start(f32[1,16,64,128]{3,2,1,0:T(8,128)S(1)} %get-tuple-element.477), channel_id=1, source_target_pairs={{0,8},{8,16},{16,24},{24,32},{32,40},{40,48},{48,56},{56,64},{64,7... | collective-permute-start | bytes 1572872 | tf_op jit(solution)/shard_map/while/body/eval_jaxpr/ppermute | solution.py:15
  296.1 8.8 %copy-start.3 = (f32[1,16,64,128]{3,2,1,0:T(8,128)S(1)}, f32[1,16,64,128]{3,2,1,0:T(8,128)}, u32[]{:S(2)}) copy-start(f32[1,16,64,128]{3,2,1,0:T(8,128)} %copy-done.2) | copy-start | bytes 1572868 | tf_op jit(solution)/shard_map/while
  305.7 14.2 %collective-permute-start = (f32[1,16,64,128]{3,2,1,0:T(8,128)S(1)}, f32[1,16,64,128]{3,2,1,0:T(8,128)S(1)}, u32[]{:S(2)}, u32[]{:S(2)}) collective-permute-start(f32[1,16,64,128]{3,2,1,0:T(8,128)S(1)} %get-tuple-element.477), channel_id=1, source_target_pairs={{0,8},{8,16},{16,24},{24,32},{32,40},{40,48},{48,56},{56,64},{64,7... | collective-permute-start | bytes 1572872 | tf_op jit(solution)/shard_map/while/body/eval_jaxpr/ppermute | solution.py:15
  311.9 8.0 %copy-start.3 = (f32[1,16,64,128]{3,2,1,0:T(8,128)S(1)}, f32[1,16,64,128]{3,2,1,0:T(8,128)}, u32[]{:S(2)}) copy-start(f32[1,16,64,128]{3,2,1,0:T(8,128)} %copy-done.2) | copy-start | bytes 1572868 | tf_op jit(solution)/shard_map/while
  320.7 13.3 %collective-permute-start = (f32[1,16,64,128]{3,2,1,0:T(8,128)S(1)}, f32[1,16,64,128]{3,2,1,0:T(8,128)S(1)}, u32[]{:S(2)}, u32[]{:S(2)}) collective-permute-start(f32[1,16,64,128]{3,2,1,0:T(8,128)S(1)} %get-tuple-element.477), channel_id=1, source_target_pairs={{0,8},{8,16},{16,24},{24,32},{32,40},{40,48},{48,56},{56,64},{64,7... | collective-permute-start | bytes 1572872 | tf_op jit(solution)/shard_map/while/body/eval_jaxpr/ppermute | solution.py:15
  327.0 7.1 %copy-start.3 = (f32[1,16,64,128]{3,2,1,0:T(8,128)S(1)}, f32[1,16,64,128]{3,2,1,0:T(8,128)}, u32[]{:S(2)}) copy-start(f32[1,16,64,128]{3,2,1,0:T(8,128)} %copy-done.2) | copy-start | bytes 1572868 | tf_op jit(solution)/shard_map/while
  334.9 12.3 %collective-permute-start = (f32[1,16,64,128]{3,2,1,0:T(8,128)S(1)}, f32[1,16,64,128]{3,2,1,0:T(8,128)S(1)}, u32[]{:S(2)}, u32[]{:S(2)}) collective-permute-start(f32[1,16,64,128]{3,2,1,0:T(8,128)S(1)} %get-tuple-element.477), channel_id=1, source_target_pairs={{0,8},{8,16},{16,24},{24,32},{32,40},{40,48},{48,56},{56,64},{64,7... | collective-permute-start | bytes 1572872 | tf_op jit(solution)/shard_map/while/body/eval_jaxpr/ppermute | solution.py:15
  412.5 37.4 %copy-start.10 = (f32[4]{0:T(128)}, f32[4]{0:T(128)S(1)}, u32[]{:S(2)}) copy-start(f32[4]{0:T(128)S(1)} %get-tuple-element.375) | copy-start | bytes 52
  412.5 38.0 %copy-start.8 = (f32[4,2]{0,1:T(2,128)}, f32[4,2]{0,1:T(2,128)S(1)}, u32[]{:S(2)}) copy-start(f32[4,2]{0,1:T(2,128)S(1)} %get-tuple-element.374) | copy-start | bytes 100
  (34 other events, 71.7 us)
where the time goes:
time: 460 us; the launch traced here: 459 us
  starting transfers between devices  141 us (31%)
  blocking collectives  108 us (23%)
  waiting for transfers between devices  100 us (22%)
  other arithmetic  31.4 us (7%)
  local copies, waits for them, and re-layouts  31.3 us (7%)
  loops' own time  28.7 us (6%)
  matrix products  16.6 us (4%)
    ppermute x19, starting transfers between devices, from_behind(): return lax.ppermute(value, axis, pairs)  141 us
    ppermute x19, waiting for transfers between devices, from_behind(): return lax.ppermute(value, axis, pairs)  100 us
    psum x2, blocking collectives, over_axes(): value = lax.psum(value, axis)  65.3 us
    all_to_all x2, blocking collectives, from_everyone(): lax.all_to_all(jnp.broadcast_to(value[None], (length, *value.shape)), axi...  43.1 us
    another operation x1, loops' own time, body(): lax.fori_loop(0, sections + groups - 1, section, initial)  23.5 us
    reduce_sum x19, other arithmetic, amplitude(): jnp.sum(b_real * c_real - b_imag * c_imag, axis=(1, 2, 3)) * factor  18.4 us
    while x76, local copies, waits for them, and re-layouts  14.3 us
  transfers between devices with their start and end apart: 19, of which 19 were waited for; matrix products, arithmetic and copies ran while one was open for 5% of the time, Pallas kernels for 0%

commit v1 on v0

--- a/solution.py
+++ b/solution.py
@@ -17,7 +17,8 @@
 
 def over_axes(value, axes):
     for axis in axes:
-        value = lax.psum(value, axis)
+        parts = lax.all_gather(value, axis)
+        value = jnp.sum(parts, axis=0)
     return value
 
 

time: 460 us -> 476 us (1.035)
  starting transfers between devices: 141 us -> 172 us
  blocking collectives: 108 us -> 88.1 us
    psum x2 -> x0, blocking collectives: 65.3 us -> none  [over_axes(): value = lax.psum(value, axis)]
    unnamed x0 -> x2, blocking collectives: none -> 64.9 us
    all_to_all x0 -> x1, starting transfers between devices: none -> 31.2 us  [from_everyone(): lax.all_to_all(jnp.broadcast_to(value[None], (length, *value.shape)), axi...]
    all_to_all x2 -> x1, blocking collectives: 43.1 us -> 12.7 us  [from_everyone(): lax.all_to_all(jnp.broadcast_to(value[None], (length, *value.shape)), axi...]
    all_gather x0 -> x2, blocking collectives: none -> 10.5 us  [over_axes(): parts = lax.all_gather(value, axis)]
  transfers between devices with their start and end apart: 19 -> 20, of which waited for: 19 -> 19; matrix products, arithmetic and copies ran while one was open for 5% -> 5% of each run, Pallas kernels for 0% -> 0%
where the time goes in v1:
time: 476 us; the launch traced here: 475 us
  starting transfers between devices  172 us (36%)
  waiting for transfers between devices  100 us (21%)
  blocking collectives  88.1 us (19%)
  local copies, waits for them, and re-layouts  34.8 us (7%)
  other arithmetic  31.5 us (7%)
  loops' own time  28.7 us (6%)
  matrix products  16.6 us (3%)
    ppermute x19, starting transfers between devices, from_behind(): return lax.ppermute(value, axis, pairs)  141 us
    ppermute x19, waiting for transfers between devices, from_behind(): return lax.ppermute(value, axis, pairs)  100 us
    unnamed x2, blocking collectives  64.9 us
    all_to_all x1, starting transfers between devices, from_everyone(): lax.all_to_all(jnp.broadcast_to(value[None], (length, *value.shape)), axi...  31.2 us
    another operation x1, loops' own time, body(): lax.fori_loop(0, sections + groups - 1, section, initial)  23.5 us
    reduce_sum x19, other arithmetic, amplitude(): jnp.sum(b_real * c_real - b_imag * c_imag, axis=(1, 2, 3)) * factor  18.4 us
    while x76, local copies, waits for them, and re-layouts  14.3 us
    all_to_all x1, blocking collectives, from_everyone(): lax.all_to_all(jnp.broadcast_to(value[None], (length, *value.shape)), axi...  12.7 us
  transfers between devices with their start and end apart: 20, of which 19 were waited for; matrix products, arithmetic and copies ran while one was open for 5% of the time, Pallas kernels for 0%

profile of v1, /device:TPU:1, one launch (start us, length us, event | category | flops | bytes accessed | tf_op | source)
XLA Modules:
  0.0 474.6 jit_solution(10498324926325785263)
XLA Ops:
  8.1 340.9 %while.18 = (s32[]{:T(128)}, f32[1,16,64,128]{3,2,1,0:T(8,128)S(1)}, f32[4,2]{0,1:T(2,128)S(1)}, f32[4]{0:T(128)S(1)}, s32[]{:T(128)}, /*index=5*/pred[]{:T(512)...) while((s32[]{:T(128)}, ...), condition=%wide.region_7.8_spmd, body=%wide.region_0.7_spmd.sunk | while | flops 404756480 | bytes 22449744 | solution.py:137
  8.9 8.9 %conditional.2 = (f32[1,16,64,128]{3,2,1,0:T(8,128)S(1)}, f32[1]{0:T(128)}) conditional(s32[]{:T(128)} %convert_element_type.12, f32[1,16,64,128]{3,2,1,0:T(8,128)S(1)} %broadcast_select_fusion.2, (f32[1,16,64,128]{3,2,1,0:T(8,128)S(1)}, f32[1,16,64,128]{3,2,1,0:T(8,128)}, f32[1,16,64,128]{3,2,1,0:T(8,128)S(1)}, s32[4,1]{0,1:T(1,128)S(1)}, s32[]{:T(128)}, ...), branch_computations={%region_1.1_spmd, %region_2.4_spmd} | conditional | flops 404101120 | bytes 13536336 | solution.py:115
  21.7 7.7 %collective-permute-done = f32[1,16,64,128]{3,2,1,0:T(8,128)S(1)} collective-permute-done((f32[1,16,64,128]{3,2,1,0:T(8,128)S(1)}, f32[1,16,64,128]{3,2,1,0:T(8,128)S(1)}, u32[]{:S(2)}, u32[]{:S(2)}) %collective-permute-start) | collective-permute-done | bytes 524320 | tf_op jit(solution)/shard_map/while/body/eval_jaxpr/ppermute | solution.py:15
  30.1 8.9 %conditional.2 = (f32[1,16,64,128]{3,2,1,0:T(8,128)S(1)}, f32[1]{0:T(128)}) conditional(s32[]{:T(128)} %convert_element_type.12, f32[1,16,64,128]{3,2,1,0:T(8,128)S(1)} %broadcast_select_fusion.2, (f32[1,16,64,128]{3,2,1,0:T(8,128)S(1)}, f32[1,16,64,128]{3,2,1,0:T(8,128)}, f32[1,16,64,128]{3,2,1,0:T(8,128)S(1)}, s32[4,1]{0,1:T(1,128)S(1)}, s32[]{:T(128)}, ...), branch_computations={%region_1.1_spmd, %region_2.4_spmd} | conditional | flops 404101120 | bytes 13536336 | solution.py:115
  45.7 6.7 %collective-permute-done = f32[1,16,64,128]{3,2,1,0:T(8,128)S(1)} collective-permute-done((f32[1,16,64,128]{3,2,1,0:T(8,128)S(1)}, f32[1,16,64,128]{3,2,1,0:T(8,128)S(1)}, u32[]{:S(2)}, u32[]{:S(2)}) %collective-permute-start) | collective-permute-done | bytes 524320 | tf_op jit(solution)/shard_map/while/body/eval_jaxpr/ppermute | solution.py:15
  53.3 8.9 %conditional.2 = (f32[1,16,64,128]{3,2,1,0:T(8,128)S(1)}, f32[1]{0:T(128)}) conditional(s32[]{:T(128)} %convert_element_type.12, f32[1,16,64,128]{3,2,1,0:T(8,128)S(1)} %broadcast_select_fusion.2, (f32[1,16,64,128]{3,2,1,0:T(8,128)S(1)}, f32[1,16,64,128]{3,2,1,0:T(8,128)}, f32[1,16,64,128]{3,2,1,0:T(8,128)S(1)}, s32[4,1]{0,1:T(1,128)S(1)}, s32[]{:T(128)}, ...), branch_computations={%region_1.1_spmd, %region_2.4_spmd} | conditional | flops 404101120 | bytes 13536336 | solution.py:115
  68.9 5.9 %collective-permute-done = f32[1,16,64,128]{3,2,1,0:T(8,128)S(1)} collective-permute-done((f32[1,16,64,128]{3,2,1,0:T(8,128)S(1)}, f32[1,16,64,128]{3,2,1,0:T(8,128)S(1)}, u32[]{:S(2)}, u32[]{:S(2)}) %collective-permute-start) | collective-permute-done | bytes 524320 | tf_op jit(solution)/shard_map/while/body/eval_jaxpr/ppermute | solution.py:15
  75.6 8.9 %conditional.2 = (f32[1,16,64,128]{3,2,1,0:T(8,128)S(1)}, f32[1]{0:T(128)}) conditional(s32[]{:T(128)} %convert_element_type.12, f32[1,16,64,128]{3,2,1,0:T(8,128)S(1)} %broadcast_select_fusion.2, (f32[1,16,64,128]{3,2,1,0:T(8,128)S(1)}, f32[1,16,64,128]{3,2,1,0:T(8,128)}, f32[1,16,64,128]{3,2,1,0:T(8,128)S(1)}, s32[4,1]{0,1:T(1,128)S(1)}, s32[]{:T(128)}, ...), branch_computations={%region_1.1_spmd, %region_2.4_spmd} | conditional | flops 404101120 | bytes 13536336 | solution.py:115
  97.1 13.1 %collective-permute-start = (f32[1,16,64,128]{3,2,1,0:T(8,128)S(1)}, f32[1,16,64,128]{3,2,1,0:T(8,128)S(1)}, u32[]{:S(2)}, u32[]{:S(2)}) collective-permute-start(f32[1,16,64,128]{3,2,1,0:T(8,128)S(1)} %get-tuple-element.487), channel_id=1, source_target_pairs={{0,8},{8,16},{16,24},{24,32},{32,40},{40,48},{48,56},{56,64},{64,7... | collective-permute-start | bytes 1572872 | tf_op jit(solution)/shard_map/while/body/eval_jaxpr/ppermute | solution.py:15
  128.7 12.0 %collective-permute-start = (f32[1,16,64,128]{3,2,1,0:T(8,128)S(1)}, f32[1,16,64,128]{3,2,1,0:T(8,128)S(1)}, u32[]{:S(2)}, u32[]{:S(2)}) collective-permute-start(f32[1,16,64,128]{3,2,1,0:T(8,128)S(1)} %get-tuple-element.487), channel_id=1, source_target_pairs={{0,8},{8,16},{16,24},{24,32},{32,40},{40,48},{48,56},{56,64},{64,7... | collective-permute-start | bytes 1572872 | tf_op jit(solution)/shard_map/while/body/eval_jaxpr/ppermute | solution.py:15
  159.8 13.7 %collective-permute-start = (f32[1,16,64,128]{3,2,1,0:T(8,128)S(1)}, f32[1,16,64,128]{3,2,1,0:T(8,128)S(1)}, u32[]{:S(2)}, u32[]{:S(2)}) collective-permute-start(f32[1,16,64,128]{3,2,1,0:T(8,128)S(1)} %get-tuple-element.487), channel_id=1, source_target_pairs={{0,8},{8,16},{16,24},{24,32},{32,40},{40,48},{48,56},{56,64},{64,7... | collective-permute-start | bytes 1572872 | tf_op jit(solution)/shard_map/while/body/eval_jaxpr/ppermute | solution.py:15
  180.4 6.2 %collective-permute-start = (f32[1,16,64,128]{3,2,1,0:T(8,128)S(1)}, f32[1,16,64,128]{3,2,1,0:T(8,128)S(1)}, u32[]{:S(2)}, u32[]{:S(2)}) collective-permute-start(f32[1,16,64,128]{3,2,1,0:T(8,128)S(1)} %get-tuple-element.487), channel_id=1, source_target_pairs={{0,8},{8,16},{16,24},{24,32},{32,40},{40,48},{48,56},{56,64},{64,7... | collective-permute-start | bytes 1572872 | tf_op jit(solution)/shard_map/while/body/eval_jaxpr/ppermute | solution.py:15
  193.6 14.8 %collective-permute-start = (f32[1,16,64,128]{3,2,1,0:T(8,128)S(1)}, f32[1,16,64,128]{3,2,1,0:T(8,128)S(1)}, u32[]{:S(2)}, u32[]{:S(2)}) collective-permute-start(f32[1,16,64,128]{3,2,1,0:T(8,128)S(1)} %get-tuple-element.487), channel_id=1, source_target_pairs={{0,8},{8,16},{16,24},{24,32},{32,40},{40,48},{48,56},{56,64},{64,7... | collective-permute-start | bytes 1572872 | tf_op jit(solution)/shard_map/while/body/eval_jaxpr/ppermute | solution.py:15
  215.3 8.1 %collective-permute-start = (f32[1,16,64,128]{3,2,1,0:T(8,128)S(1)}, f32[1,16,64,128]{3,2,1,0:T(8,128)S(1)}, u32[]{:S(2)}, u32[]{:S(2)}) collective-permute-start(f32[1,16,64,128]{3,2,1,0:T(8,128)S(1)} %get-tuple-element.487), channel_id=1, source_target_pairs={{0,8},{8,16},{16,24},{24,32},{32,40},{40,48},{48,56},{56,64},{64,7... | collective-permute-start | bytes 1572872 | tf_op jit(solution)/shard_map/while/body/eval_jaxpr/ppermute | solution.py:15
  225.9 5.9 %collective-permute-done = f32[1,16,64,128]{3,2,1,0:T(8,128)S(1)} collective-permute-done((f32[1,16,64,128]{3,2,1,0:T(8,128)S(1)}, f32[1,16,64,128]{3,2,1,0:T(8,128)S(1)}, u32[]{:S(2)}, u32[]{:S(2)}) %collective-permute-start) | collective-permute-done | bytes 524320 | tf_op jit(solution)/shard_map/while/body/eval_jaxpr/ppermute | solution.py:15
  239.4 6.6 %collective-permute-done = f32[1,16,64,128]{3,2,1,0:T(8,128)S(1)} collective-permute-done((f32[1,16,64,128]{3,2,1,0:T(8,128)S(1)}, f32[1,16,64,128]{3,2,1,0:T(8,128)S(1)}, u32[]{:S(2)}, u32[]{:S(2)}) %collective-permute-start) | collective-permute-done | bytes 524320 | tf_op jit(solution)/shard_map/while/body/eval_jaxpr/ppermute | solution.py:15
  246.9 17.0 %collective-permute-start = (f32[1,16,64,128]{3,2,1,0:T(8,128)S(1)}, f32[1,16,64,128]{3,2,1,0:T(8,128)S(1)}, u32[]{:S(2)}, u32[]{:S(2)}) collective-permute-start(f32[1,16,64,128]{3,2,1,0:T(8,128)S(1)} %get-tuple-element.487), channel_id=1, source_target_pairs={{0,8},{8,16},{16,24},{24,32},{32,40},{40,48},{48,56},{56,64},{64,7... | collective-permute-start | bytes 1572872 | tf_op jit(solution)/shard_map/while/body/eval_jaxpr/ppermute | solution.py:15
  266.4 8.6 %collective-permute-done = f32[1,16,64,128]{3,2,1,0:T(8,128)S(1)} collective-permute-done((f32[1,16,64,128]{3,2,1,0:T(8,128)S(1)}, f32[1,16,64,128]{3,2,1,0:T(8,128)S(1)}, u32[]{:S(2)}, u32[]{:S(2)}) %collective-permute-start) | collective-permute-done | bytes 524320 | tf_op jit(solution)/shard_map/while/body/eval_jaxpr/ppermute | solution.py:15
  275.8 6.2 %collective-permute-start = (f32[1,16,64,128]{3,2,1,0:T(8,128)S(1)}, f32[1,16,64,128]{3,2,1,0:T(8,128)S(1)}, u32[]{:S(2)}, u32[]{:S(2)}) collective-permute-start(f32[1,16,64,128]{3,2,1,0:T(8,128)S(1)} %get-tuple-element.487), channel_id=1, source_target_pairs={{0,8},{8,16},{16,24},{24,32},{32,40},{40,48},{48,56},{56,64},{64,7... | collective-permute-start | bytes 1572872 | tf_op jit(solution)/shard_map/while/body/eval_jaxpr/ppermute | solution.py:15
  284.5 7.4 %collective-permute-done = f32[1,16,64,128]{3,2,1,0:T(8,128)S(1)} collective-permute-done((f32[1,16,64,128]{3,2,1,0:T(8,128)S(1)}, f32[1,16,64,128]{3,2,1,0:T(8,128)S(1)}, u32[]{:S(2)}, u32[]{:S(2)}) %collective-permute-start) | collective-permute-done | bytes 524320 | tf_op jit(solution)/shard_map/while/body/eval_jaxpr/ppermute | solution.py:15
  292.8 5.1 %collective-permute-start = (f32[1,16,64,128]{3,2,1,0:T(8,128)S(1)}, f32[1,16,64,128]{3,2,1,0:T(8,128)S(1)}, u32[]{:S(2)}, u32[]{:S(2)}) collective-permute-start(f32[1,16,64,128]{3,2,1,0:T(8,128)S(1)} %get-tuple-element.487), channel_id=1, source_target_pairs={{0,8},{8,16},{16,24},{24,32},{32,40},{40,48},{48,56},{56,64},{64,7... | collective-permute-start | bytes 1572872 | tf_op jit(solution)/shard_map/while/body/eval_jaxpr/ppermute | solution.py:15
  300.4 6.3 %collective-permute-done = f32[1,16,64,128]{3,2,1,0:T(8,128)S(1)} collective-permute-done((f32[1,16,64,128]{3,2,1,0:T(8,128)S(1)}, f32[1,16,64,128]{3,2,1,0:T(8,128)S(1)}, u32[]{:S(2)}, u32[]{:S(2)}) %collective-permute-start) | collective-permute-done | bytes 524320 | tf_op jit(solution)/shard_map/while/body/eval_jaxpr/ppermute | solution.py:15
  307.5 6.2 %collective-permute-start = (f32[1,16,64,128]{3,2,1,0:T(8,128)S(1)}, f32[1,16,64,128]{3,2,1,0:T(8,128)S(1)}, u32[]{:S(2)}, u32[]{:S(2)}) collective-permute-start(f32[1,16,64,128]{3,2,1,0:T(8,128)S(1)} %get-tuple-element.487), channel_id=1, source_target_pairs={{0,8},{8,16},{16,24},{24,32},{32,40},{40,48},{48,56},{56,64},{64,7... | collective-permute-start | bytes 1572872 | tf_op jit(solution)/shard_map/while/body/eval_jaxpr/ppermute | solution.py:15
  316.3 5.4 %collective-permute-done = f32[1,16,64,128]{3,2,1,0:T(8,128)S(1)} collective-permute-done((f32[1,16,64,128]{3,2,1,0:T(8,128)S(1)}, f32[1,16,64,128]{3,2,1,0:T(8,128)S(1)}, u32[]{:S(2)}, u32[]{:S(2)}) %collective-permute-start) | collective-permute-done | bytes 524320 | tf_op jit(solution)/shard_map/while/body/eval_jaxpr/ppermute | solution.py:15
  322.5 6.2 %collective-permute-start = (f32[1,16,64,128]{3,2,1,0:T(8,128)S(1)}, f32[1,16,64,128]{3,2,1,0:T(8,128)S(1)}, u32[]{:S(2)}, u32[]{:S(2)}) collective-permute-start(f32[1,16,64,128]{3,2,1,0:T(8,128)S(1)} %get-tuple-element.487), channel_id=1, source_target_pairs={{0,8},{8,16},{16,24},{24,32},{32,40},{40,48},{48,56},{56,64},{64,7... | collective-permute-start | bytes 1572872 | tf_op jit(solution)/shard_map/while/body/eval_jaxpr/ppermute | solution.py:15
  336.7 6.2 %collective-permute-start = (f32[1,16,64,128]{3,2,1,0:T(8,128)S(1)}, f32[1,16,64,128]{3,2,1,0:T(8,128)S(1)}, u32[]{:S(2)}, u32[]{:S(2)}) collective-permute-start(f32[1,16,64,128]{3,2,1,0:T(8,128)S(1)} %get-tuple-element.487), channel_id=1, source_target_pairs={{0,8},{8,16},{16,24},{24,32},{32,40},{40,48},{48,56},{56,64},{64,7... | collective-permute-start | bytes 1572872 | tf_op jit(solution)/shard_map/while/body/eval_jaxpr/ppermute | solution.py:15
  349.2 54.1 %all-reduce.1 = f32[16]{0:T(128)S(1)} all-reduce(f32[16]{0:T(128)S(1)} %dynamic-update-slice.8), channel_id=4, replica_groups=mesh['col_0'=4,'col_1'=4,'cuts'=8] {'col_0'}, use_global_device_ids=true, to_apply=%add.1 | all-reduce | flops 16 | bytes 128
  405.5 10.8 %all-reduce.2 = f32[16]{0:T(128)S(1)} all-reduce(f32[16]{0:T(128)S(1)} %dynamic-update-slice.9), channel_id=5, replica_groups=mesh['col_0'=4,'col_1'=4,'cuts'=8] {'col_1'}, use_global_device_ids=true, to_apply=%add.2 | all-reduce | flops 16 | bytes 128
  418.3 31.2 %all-to-all-start = ((f32[8,1,1]{2,1,0:T(1,128)}), f32[8,1,1]{2,1,0:T(1,128)S(1)}, u32[]{:S(2)}, u32[]{:S(2)}) async-start(f32[8,1,1]{2,1,0:T(1,128)} %broadcast_in_dim.43), calls=%async_computation | async-start | bytes 8192 | tf_op jit(solution)/shard_map/all_to_all | solution.py:27
  449.5 5.2 %all-gather.4 = f32[4,4,2]{1,2,0:T(2,128)S(1)} all-gather(f32[1,4,2]{1,2,0:T(2,128)S(1)} %bitcast.108), channel_id=2, replica_groups=mesh['col_0'=4,'col_1'=4,'cuts'=8] {'col_0'}, dimensions={0}, use_global_device_ids=true | all-gather | bytes 160 | tf_op jit(solution)/shard_map/all_gather | solution.py:20
  454.7 5.2 %all-gather.5 = f32[4,4,2]{1,2,0:T(2,128)S(1)} all-gather(f32[1,4,2]{1,2,0:T(2,128)S(1)} %bitcast.109), channel_id=3, replica_groups=mesh['col_0'=4,'col_1'=4,'cuts'=8] {'col_1'}, dimensions={0}, use_global_device_ids=true | all-gather | bytes 160 | tf_op jit(solution)/shard_map/all_gather | solution.py:20
  461.4 12.7 %all_to_all.12 = f32[8,1,2]{2,1,0:T(1,128)S(1)} all-to-all(f32[8,1,2]{2,1,0:T(1,128)S(1)} %broadcast_in_dim.44), channel_id=1, replica_groups=mesh['col_0'=4,'col_1'=4,'cuts'=8] {'cuts'}, dimensions={0} | all-to-all | bytes 128 | tf_op jit(solution)/shard_map/all_to_all | solution.py:27
  (298 shorter events, 149.0 us)
Async XLA Ops:
  17.9 11.5 %collective-permute-start = (f32[1,16,64,128]{3,2,1,0:T(8,128)S(1)}, f32[1,16,64,128]{3,2,1,0:T(8,128)S(1)}, u32[]{:S(2)}, u32[]{:S(2)}) collective-permute-start(f32[1,16,64,128]{3,2,1,0:T(8,128)S(1)} %get-tuple-element.487), channel_id=1, source_target_pairs={{0,8},{8,16},{16,24},{24,32},{32,40},{40,48},{48,56},{56,64},{64,7... | collective-permute-start | bytes 1572872 | tf_op jit(solution)/shard_map/while/body/eval_jaxpr/ppermute | solution.py:15
  19.2 10.1 %copy-start.3 = (f32[1,16,64,128]{3,2,1,0:T(8,128)S(1)}, f32[1,16,64,128]{3,2,1,0:T(8,128)}, u32[]{:S(2)}) copy-start(f32[1,16,64,128]{3,2,1,0:T(8,128)} %copy-done.2) | copy-start | bytes 1572868 | tf_op jit(solution)/shard_map/while
  39.1 13.4 %collective-permute-start = (f32[1,16,64,128]{3,2,1,0:T(8,128)S(1)}, f32[1,16,64,128]{3,2,1,0:T(8,128)S(1)}, u32[]{:S(2)}, u32[]{:S(2)}) collective-permute-start(f32[1,16,64,128]{3,2,1,0:T(8,128)S(1)} %get-tuple-element.487), channel_id=1, source_target_pairs={{0,8},{8,16},{16,24},{24,32},{32,40},{40,48},{48,56},{56,64},{64,7... | collective-permute-start | bytes 1572872 | tf_op jit(solution)/shard_map/while/body/eval_jaxpr/ppermute | solution.py:15
  43.2 9.3 %copy-start.3 = (f32[1,16,64,128]{3,2,1,0:T(8,128)S(1)}, f32[1,16,64,128]{3,2,1,0:T(8,128)}, u32[]{:S(2)}) copy-start(f32[1,16,64,128]{3,2,1,0:T(8,128)} %copy-done.2) | copy-start | bytes 1572868 | tf_op jit(solution)/shard_map/while
  62.2 12.6 %collective-permute-start = (f32[1,16,64,128]{3,2,1,0:T(8,128)S(1)}, f32[1,16,64,128]{3,2,1,0:T(8,128)S(1)}, u32[]{:S(2)}, u32[]{:S(2)}) collective-permute-start(f32[1,16,64,128]{3,2,1,0:T(8,128)S(1)} %get-tuple-element.487), channel_id=1, source_target_pairs={{0,8},{8,16},{16,24},{24,32},{32,40},{40,48},{48,56},{56,64},{64,7... | collective-permute-start | bytes 1572872 | tf_op jit(solution)/shard_map/while/body/eval_jaxpr/ppermute | solution.py:15
  66.4 8.4 %copy-start.3 = (f32[1,16,64,128]{3,2,1,0:T(8,128)S(1)}, f32[1,16,64,128]{3,2,1,0:T(8,128)}, u32[]{:S(2)}) copy-start(f32[1,16,64,128]{3,2,1,0:T(8,128)} %copy-done.2) | copy-start | bytes 1572868 | tf_op jit(solution)/shard_map/while
  84.5 11.7 %collective-permute-start = (f32[1,16,64,128]{3,2,1,0:T(8,128)S(1)}, f32[1,16,64,128]{3,2,1,0:T(8,128)S(1)}, u32[]{:S(2)}, u32[]{:S(2)}) collective-permute-start(f32[1,16,64,128]{3,2,1,0:T(8,128)S(1)} %get-tuple-element.487), channel_id=1, source_target_pairs={{0,8},{8,16},{16,24},{24,32},{32,40},{40,48},{48,56},{56,64},{64,7... | collective-permute-start | bytes 1572872 | tf_op jit(solution)/shard_map/while/body/eval_jaxpr/ppermute | solution.py:15
  88.7 7.6 %copy-start.3 = (f32[1,16,64,128]{3,2,1,0:T(8,128)S(1)}, f32[1,16,64,128]{3,2,1,0:T(8,128)}, u32[]{:S(2)}) copy-start(f32[1,16,64,128]{3,2,1,0:T(8,128)} %copy-done.2) | copy-start | bytes 1572868 | tf_op jit(solution)/shard_map/while
  97.1 19.8 %collective-permute-start = (f32[1,16,64,128]{3,2,1,0:T(8,128)S(1)}, f32[1,16,64,128]{3,2,1,0:T(8,128)S(1)}, u32[]{:S(2)}, u32[]{:S(2)}) collective-permute-start(f32[1,16,64,128]{3,2,1,0:T(8,128)S(1)} %get-tuple-element.487), channel_id=1, source_target_pairs={{0,8},{8,16},{16,24},{24,32},{32,40},{40,48},{48,56},{56,64},{64,7... | collective-permute-start | bytes 1572872 | tf_op jit(solution)/shard_map/while/body/eval_jaxpr/ppermute | solution.py:15
  117.6 10.2 %collective-permute-start = (f32[1,16,64,128]{3,2,1,0:T(8,128)S(1)}, f32[1,16,64,128]{3,2,1,0:T(8,128)S(1)}, u32[]{:S(2)}, u32[]{:S(2)}) collective-permute-start(f32[1,16,64,128]{3,2,1,0:T(8,128)S(1)} %get-tuple-element.487), channel_id=1, source_target_pairs={{0,8},{8,16},{16,24},{24,32},{32,40},{40,48},{48,56},{56,64},{64,7... | collective-permute-start | bytes 1572872 | tf_op jit(solution)/shard_map/while/body/eval_jaxpr/ppermute | solution.py:15
  128.7 18.1 %collective-permute-start = (f32[1,16,64,128]{3,2,1,0:T(8,128)S(1)}, f32[1,16,64,128]{3,2,1,0:T(8,128)S(1)}, u32[]{:S(2)}, u32[]{:S(2)}) collective-permute-start(f32[1,16,64,128]{3,2,1,0:T(8,128)S(1)} %get-tuple-element.487), channel_id=1, source_target_pairs={{0,8},{8,16},{16,24},{24,32},{32,40},{40,48},{48,56},{56,64},{64,7... | collective-permute-start | bytes 1572872 | tf_op jit(solution)/shard_map/while/body/eval_jaxpr/ppermute | solution.py:15
  147.6 11.4 %collective-permute-start = (f32[1,16,64,128]{3,2,1,0:T(8,128)S(1)}, f32[1,16,64,128]{3,2,1,0:T(8,128)S(1)}, u32[]{:S(2)}, u32[]{:S(2)}) collective-permute-start(f32[1,16,64,128]{3,2,1,0:T(8,128)S(1)} %get-tuple-element.487), channel_id=1, source_target_pairs={{0,8},{8,16},{16,24},{24,32},{32,40},{40,48},{48,56},{56,64},{64,7... | collective-permute-start | bytes 1572872 | tf_op jit(solution)/shard_map/while/body/eval_jaxpr/ppermute | solution.py:15
  159.8 19.8 %collective-permute-start = (f32[1,16,64,128]{3,2,1,0:T(8,128)S(1)}, f32[1,16,64,128]{3,2,1,0:T(8,128)S(1)}, u32[]{:S(2)}, u32[]{:S(2)}) collective-permute-start(f32[1,16,64,128]{3,2,1,0:T(8,128)S(1)} %get-tuple-element.487), channel_id=1, source_target_pairs={{0,8},{8,16},{16,24},{24,32},{32,40},{40,48},{48,56},{56,64},{64,7... | collective-permute-start | bytes 1572872 | tf_op jit(solution)/shard_map/while/body/eval_jaxpr/ppermute | solution.py:15
  180.4 12.4 %collective-permute-start = (f32[1,16,64,128]{3,2,1,0:T(8,128)S(1)}, f32[1,16,64,128]{3,2,1,0:T(8,128)S(1)}, u32[]{:S(2)}, u32[]{:S(2)}) collective-permute-start(f32[1,16,64,128]{3,2,1,0:T(8,128)S(1)} %get-tuple-element.487), channel_id=1, source_target_pairs={{0,8},{8,16},{16,24},{24,32},{32,40},{40,48},{48,56},{56,64},{64,7... | collective-permute-start | bytes 1572872 | tf_op jit(solution)/shard_map/while/body/eval_jaxpr/ppermute | solution.py:15
  193.6 20.9 %collective-permute-start = (f32[1,16,64,128]{3,2,1,0:T(8,128)S(1)}, f32[1,16,64,128]{3,2,1,0:T(8,128)S(1)}, u32[]{:S(2)}, u32[]{:S(2)}) collective-permute-start(f32[1,16,64,128]{3,2,1,0:T(8,128)S(1)} %get-tuple-element.487), channel_id=1, source_target_pairs={{0,8},{8,16},{16,24},{24,32},{32,40},{40,48},{48,56},{56,64},{64,7... | collective-permute-start | bytes 1572872 | tf_op jit(solution)/shard_map/while/body/eval_jaxpr/ppermute | solution.py:15
  215.3 16.5 %collective-permute-start = (f32[1,16,64,128]{3,2,1,0:T(8,128)S(1)}, f32[1,16,64,128]{3,2,1,0:T(8,128)S(1)}, u32[]{:S(2)}, u32[]{:S(2)}) collective-permute-start(f32[1,16,64,128]{3,2,1,0:T(8,128)S(1)} %get-tuple-element.487), channel_id=1, source_target_pairs={{0,8},{8,16},{16,24},{24,32},{32,40},{40,48},{48,56},{56,64},{64,7... | collective-permute-start | bytes 1572872 | tf_op jit(solution)/shard_map/while/body/eval_jaxpr/ppermute | solution.py:15
  223.4 8.4 %copy-start.3 = (f32[1,16,64,128]{3,2,1,0:T(8,128)S(1)}, f32[1,16,64,128]{3,2,1,0:T(8,128)}, u32[]{:S(2)}) copy-start(f32[1,16,64,128]{3,2,1,0:T(8,128)} %copy-done.2) | copy-start | bytes 1572868 | tf_op jit(solution)/shard_map/while
  232.7 13.4 %collective-permute-start = (f32[1,16,64,128]{3,2,1,0:T(8,128)S(1)}, f32[1,16,64,128]{3,2,1,0:T(8,128)S(1)}, u32[]{:S(2)}, u32[]{:S(2)}) collective-permute-start(f32[1,16,64,128]{3,2,1,0:T(8,128)S(1)} %get-tuple-element.487), channel_id=1, source_target_pairs={{0,8},{8,16},{16,24},{24,32},{32,40},{40,48},{48,56},{56,64},{64,7... | collective-permute-start | bytes 1572872 | tf_op jit(solution)/shard_map/while/body/eval_jaxpr/ppermute | solution.py:15
  236.9 9.2 %copy-start.3 = (f32[1,16,64,128]{3,2,1,0:T(8,128)S(1)}, f32[1,16,64,128]{3,2,1,0:T(8,128)}, u32[]{:S(2)}) copy-start(f32[1,16,64,128]{3,2,1,0:T(8,128)} %copy-done.2) | copy-start | bytes 1572868 | tf_op jit(solution)/shard_map/while
  246.9 28.1 %collective-permute-start = (f32[1,16,64,128]{3,2,1,0:T(8,128)S(1)}, f32[1,16,64,128]{3,2,1,0:T(8,128)S(1)}, u32[]{:S(2)}, u32[]{:S(2)}) collective-permute-start(f32[1,16,64,128]{3,2,1,0:T(8,128)S(1)} %get-tuple-element.487), channel_id=1, source_target_pairs={{0,8},{8,16},{16,24},{24,32},{32,40},{40,48},{48,56},{56,64},{64,7... | collective-permute-start | bytes 1572872 | tf_op jit(solution)/shard_map/while/body/eval_jaxpr/ppermute | solution.py:15
  263.9 11.1 %copy-start.3 = (f32[1,16,64,128]{3,2,1,0:T(8,128)S(1)}, f32[1,16,64,128]{3,2,1,0:T(8,128)}, u32[]{:S(2)}) copy-start(f32[1,16,64,128]{3,2,1,0:T(8,128)} %copy-done.2) | copy-start | bytes 1572868 | tf_op jit(solution)/shard_map/while
  275.8 16.2 %collective-permute-start = (f32[1,16,64,128]{3,2,1,0:T(8,128)S(1)}, f32[1,16,64,128]{3,2,1,0:T(8,128)S(1)}, u32[]{:S(2)}, u32[]{:S(2)}) collective-permute-start(f32[1,16,64,128]{3,2,1,0:T(8,128)S(1)} %get-tuple-element.487), channel_id=1, source_target_pairs={{0,8},{8,16},{16,24},{24,32},{32,40},{40,48},{48,56},{56,64},{64,7... | collective-permute-start | bytes 1572872 | tf_op jit(solution)/shard_map/while/body/eval_jaxpr/ppermute | solution.py:15
  282.0 10.0 %copy-start.3 = (f32[1,16,64,128]{3,2,1,0:T(8,128)S(1)}, f32[1,16,64,128]{3,2,1,0:T(8,128)}, u32[]{:S(2)}) copy-start(f32[1,16,64,128]{3,2,1,0:T(8,128)} %copy-done.2) | copy-start | bytes 1572868 | tf_op jit(solution)/shard_map/while
  292.8 13.9 %collective-permute-start = (f32[1,16,64,128]{3,2,1,0:T(8,128)S(1)}, f32[1,16,64,128]{3,2,1,0:T(8,128)S(1)}, u32[]{:S(2)}, u32[]{:S(2)}) collective-permute-start(f32[1,16,64,128]{3,2,1,0:T(8,128)S(1)} %get-tuple-element.487), channel_id=1, source_target_pairs={{0,8},{8,16},{16,24},{24,32},{32,40},{40,48},{48,56},{56,64},{64,7... | collective-permute-start | bytes 1572872 | tf_op jit(solution)/shard_map/while/body/eval_jaxpr/ppermute | solution.py:15
  297.9 8.8 %copy-start.3 = (f32[1,16,64,128]{3,2,1,0:T(8,128)S(1)}, f32[1,16,64,128]{3,2,1,0:T(8,128)}, u32[]{:S(2)}) copy-start(f32[1,16,64,128]{3,2,1,0:T(8,128)} %copy-done.2) | copy-start | bytes 1572868 | tf_op jit(solution)/shard_map/while
  307.5 14.2 %collective-permute-start = (f32[1,16,64,128]{3,2,1,0:T(8,128)S(1)}, f32[1,16,64,128]{3,2,1,0:T(8,128)S(1)}, u32[]{:S(2)}, u32[]{:S(2)}) collective-permute-start(f32[1,16,64,128]{3,2,1,0:T(8,128)S(1)} %get-tuple-element.487), channel_id=1, source_target_pairs={{0,8},{8,16},{16,24},{24,32},{32,40},{40,48},{48,56},{56,64},{64,7... | collective-permute-start | bytes 1572872 | tf_op jit(solution)/shard_map/while/body/eval_jaxpr/ppermute | solution.py:15
  313.8 8.0 %copy-start.3 = (f32[1,16,64,128]{3,2,1,0:T(8,128)S(1)}, f32[1,16,64,128]{3,2,1,0:T(8,128)}, u32[]{:S(2)}) copy-start(f32[1,16,64,128]{3,2,1,0:T(8,128)} %copy-done.2) | copy-start | bytes 1572868 | tf_op jit(solution)/shard_map/while
  322.5 13.3 %collective-permute-start = (f32[1,16,64,128]{3,2,1,0:T(8,128)S(1)}, f32[1,16,64,128]{3,2,1,0:T(8,128)S(1)}, u32[]{:S(2)}, u32[]{:S(2)}) collective-permute-start(f32[1,16,64,128]{3,2,1,0:T(8,128)S(1)} %get-tuple-element.487), channel_id=1, source_target_pairs={{0,8},{8,16},{16,24},{24,32},{32,40},{40,48},{48,56},{56,64},{64,7... | collective-permute-start | bytes 1572872 | tf_op jit(solution)/shard_map/while/body/eval_jaxpr/ppermute | solution.py:15
  328.8 7.1 %copy-start.3 = (f32[1,16,64,128]{3,2,1,0:T(8,128)S(1)}, f32[1,16,64,128]{3,2,1,0:T(8,128)}, u32[]{:S(2)}) copy-start(f32[1,16,64,128]{3,2,1,0:T(8,128)} %copy-done.2) | copy-start | bytes 1572868 | tf_op jit(solution)/shard_map/while
  336.7 12.3 %collective-permute-start = (f32[1,16,64,128]{3,2,1,0:T(8,128)S(1)}, f32[1,16,64,128]{3,2,1,0:T(8,128)S(1)}, u32[]{:S(2)}, u32[]{:S(2)}) collective-permute-start(f32[1,16,64,128]{3,2,1,0:T(8,128)S(1)} %get-tuple-element.487), channel_id=1, source_target_pairs={{0,8},{8,16},{16,24},{24,32},{32,40},{40,48},{48,56},{56,64},{64,7... | collective-permute-start | bytes 1572872 | tf_op jit(solution)/shard_map/while/body/eval_jaxpr/ppermute | solution.py:15
  416.4 44.2 %copy-start.9 = (f32[4]{0:T(128)}, f32[4]{0:T(128)S(1)}, u32[]{:S(2)}) copy-start(f32[4]{0:T(128)S(1)} %reduce_sum.79) | copy-start | bytes 52
  418.3 41.7 %all-to-all-start = ((f32[8,1,1]{2,1,0:T(1,128)}), f32[8,1,1]{2,1,0:T(1,128)S(1)}, u32[]{:S(2)}, u32[]{:S(2)}) async-start(f32[8,1,1]{2,1,0:T(1,128)} %broadcast_in_dim.43), calls=%async_computation | async-start | bytes 8192 | tf_op jit(solution)/shard_map/all_to_all | solution.py:27
  (37 other events, 75.9 us)
